TPU v7x, 32 devices: a whole 2x2x4 slice. The times are simulated.
32 devices in a mesh: space: 4 (over y, x), dp: 8 (over z, core).
Axes of the slice: x: 2, y: 2, z: 4, core: 2. Of those that a mesh axis runs over, the one named last changes fastest.
Arguments:
- mixed_two: bfloat16 [8, 16, 180, 768], P('dp', 'space'), may hold values from -6 to 6
- input_two: bfloat16 [8, 16, 180, 768], P('dp', 'space'), may hold values from -6 to 6
- cotangent: bfloat16 [8, 16, 180, 768], P('dp', 'space'), may hold values from -6 to 6
- w_in_two: bfloat16 [3072, 768], replicated, may hold values from -0.21875 to 0.21875
- w_out_two: bfloat16 [3072, 768], replicated, may hold values from -0.109375 to 0.109375
- kernel_two: bfloat16 [9, 768], replicated, may hold values from -2 to 2
- mixed_one: bfloat16 [8, 16, 180, 768], P('dp', 'space'), may hold values from -6 to 6
- w_in_one: bfloat16 [3072, 768], replicated, may hold values from -0.21875 to 0.21875
- w_out_one: bfloat16 [3072, 768], replicated, may hold values from -0.109375 to 0.109375
- kernel_one: bfloat16 [9, 768], replicated, may hold values from -2 to 2
Outputs:
- input_grad: bfloat16 [8, 16, 180, 768], P('dp', 'space')
- grad_w_in: float32 [3072, 768], P('dp')
- grad_w_out: float32 [3072, 768], P('dp')
- grad_kernel: float32 [9, 768], replicated
All inputs are finite; a program needn't handle non-finite values.
Results may differ from a plain program's by a relative error of at most 0.02.
Values may be sent and summed in bfloat16 or wider, within the bound.
A program may use at most 192 MiB of HBM per device.

v0:
```python
import functools
import math

import jax
import jax.numpy as jnp
from jax import lax
from jax.experimental import pallas as pl
from jax.experimental.pallas import tpu as pltpu
from jax.sharding import PartitionSpec as P

MESH = pl.DeviceIdType.MESH
F32 = jnp.float32
BF16 = jnp.bfloat16
GELU_C = math.sqrt(2.0 / math.pi)
GELU_D = 0.044715 * GELU_C
NT = (((1,), (1,)), ((), ()))
NN = (((1,), (0,)), ((), ()))
TN = (((0,), (0,)), ((), ()))
LANES = 128
STREAMS = 3
COMM = True


def dot(a, b, dims):
    return lax.dot_general(a, b, dims, preferred_element_type=F32)


def gelu_slope_parts(v):
    cube = GELU_D * (v * v)
    t = jnp.tanh(v * (cube + GELU_C))
    p = 1.0 + t
    act = (0.5 * v) * p
    slope = 0.5 * p + act * (1.0 - t) * (3.0 * cube + GELU_C)
    return act, slope


def bits_of(n):
    return (n - 1).bit_length()


def my_bit(index, bit):
    return (index // (1 << bit)) % 2


def flip(index, bit):
    return index + (1 << bit) * (1 - 2 * my_bit(index, bit))


def rolled(row, shift):
    if shift == 0:
        return row
    if shift == 1:
        return jnp.concatenate([row[-1:], row[:-1]], axis=0)
    return jnp.concatenate([row[1:], row[:1]], axis=0)


class Plan:
    def __init__(self, dp, space, hidden, width):
        self.dp, self.space = dp, space
        self.db, self.sb = bits_of(dp), bits_of(space)
        self.width = width
        rows = hidden // (dp * space)
        self.piece = next(q for q in (16, 8, rows) if rows % q == 0)
        self.chunks = rows // self.piece
        self.lanes = width // STREAMS
        spaces = [("space", b) for b in range(self.sb)]
        rest = [("dp", b) for b in range(1, self.db)]
        self.orders = [spaces + rest, spaces[::-1] + rest, rest + spaces]
        self.stages = self.sb + self.db - 1

    def labels(self):
        return [("dp", b) for b in reversed(range(self.db))] + [
            ("space", b) for b in reversed(range(self.sb))
        ]


def kernel(
    plan, shape, inv_batch,
    mixed_two, input_two, cotangent, w_in_two, w_out_two, kernel_two, mixed_one, w_in_one, w_out_one, kernel_one,
    out_ref, grads_ref, taps_out,
    raw_mixed, raw_input, raw_cot, raw_one,
    mixed, cot, early, w_in, w_out, w_late, act_t, pg_t, mix_acc, mix_row, grad_two, slope,
    halo_late, halo_early, taps, taps_in, term, final, *rest,
):
    stage_in = rest[: plan.stages + 1]
    (
        load_sem, weight_sem, late_sem, out_sem, own_sem,
        send_sem, recv_sem, gsend_sem, grecv_sem, hsend_sem, hrecv_sem, tsend_sem, trecv_sem,
    ) = rest[plan.stages + 1 :]
    rows, cols, width = shape
    pad = mixed.shape[1]
    tokens = rows * pad
    K = plan.chunks
    F = w_in.shape[0] * w_in.shape[2]
    dpi, spi = lax.axis_index("dp"), lax.axis_index("space")
    where = {"dp": dpi, "space": spi}
    labels = plan.labels()
    order = [0, rows - 1] + list(range(1, rows - 1))
    place = {r: n for n, r in enumerate(order)}

    loads = [
        pltpu.make_async_copy(src.at[0], dst, load_sem.at[n])
        for n, (src, dst) in enumerate(
            [(mixed_two, raw_mixed), (cotangent, raw_cot), (mixed_one, raw_one), (input_two, raw_input)]
        )
    ]

    def weight_load(k, which):
        src, dst = ((w_in_two, w_in), (w_out_two, w_out))[which]
        return pltpu.make_async_copy(src.at[:, k], dst.at[:, k], weight_sem.at[which, k])

    late_loads = [
        pltpu.make_async_copy(w_in_one, w_late, late_sem.at[0]),
        pltpu.make_async_copy(w_out_one, w_out, late_sem.at[1]),
    ]
    loads[0].start()
    weight_load(0, 0).start()
    loads[1].start()
    weight_load(0, 1).start()
    for k in range(1, K):
        weight_load(k, 0).start()
        weight_load(k, 1).start()
    loads[2].start()
    loads[3].start()
    late_loads[0].start()

    peers = [{"dp": flip(dpi, b)} for b in range(plan.db)]

    def across(offset):
        other = spi
        for b in range(plan.sb):
            if (offset >> b) & 1:
                other = flip(other, b)
        return other

    peers += [{"space": across(o)} for o in range(1, plan.space)]
    if COMM:
        barrier = pltpu.get_barrier_semaphore()
        for peer in peers:
            pl.semaphore_signal(barrier, inc=1, device_id=peer, device_id_type=MESH)

    zeros = jnp.zeros((16, width), BF16)
    for r in range(rows):
        mixed[r, pl.ds(pad - 16, 16)] = zeros
        cot[r, pl.ds(pad - 16, 16)] = zeros
        early[r, pl.ds(pad - 16, 16)] = zeros
        grad_two[r, pl.ds(pad - 16, 16)] = zeros
    mix_acc[...] = jnp.zeros_like(mix_acc)
    for halo in (halo_late, halo_early):
        pl.when(spi == 0)(lambda halo=halo: halo.__setitem__(0, jnp.zeros(halo.shape[1:], BF16)))
        pl.when(spi == plan.space - 1)(lambda halo=halo: halo.__setitem__(1, jnp.zeros(halo.shape[1:], BF16)))

    if COMM:
        pl.semaphore_wait(barrier, len(peers))

    loads[0].wait()
    for r in range(rows):
        mixed[r, pl.ds(0, cols)] = raw_mixed[r]
    loads[1].wait()
    for r in range(rows):
        cot[r, pl.ds(0, cols)] = raw_cot[r]

    def half(done, now, value):
        index = []
        for label in labels:
            if label in done:
                index.append(my_bit(where[label[0]], label[1]))
            elif label == now:
                index.append(value)
            else:
                index.append(slice(None))
        return tuple(index)

    def exchange(k, stage, stream):
        if stage == 0:
            now, done, streams = ("dp", 0), [], slice(None)
            dst = stage_in[0].at[k]
        else:
            now = plan.orders[stream][stage - 1]
            done, streams = [("dp", 0)] + plan.orders[stream][: stage - 1], stream
            dst = stage_in[stage].at[k, stream]
        mine = my_bit(where[now[0]], now[1])
        src = term.at[(k, streams, slice(None)) + half(done, now, 1 - mine)]
        kept = (k, streams, slice(None)) + half(done, now, mine)
        copy = pltpu.make_async_remote_copy(
            src_ref=src,
            dst_ref=dst,
            send_sem=send_sem.at[k, stage, stream],
            recv_sem=recv_sem.at[k, stage, stream],
            device_id={now[0]: flip(where[now[0]], now[1])},
            device_id_type=MESH,
        )
        return copy, kept, dst

    def gather(k, offset):
        return pltpu.make_async_remote_copy(
            src_ref=final.at[k],
            dst_ref=grads_ref.at[k, spi],
            send_sem=gsend_sem.at[k, offset - 1],
            recv_sem=grecv_sem.at[k, offset - 1],
            device_id={"space": across(offset)},
            device_id_type=MESH,
        )

    def own(k):
        return pltpu.make_async_copy(final.at[k], grads_ref.at[k, spi], own_sem.at[k])

    def streams_of(stage):
        return range(1 if stage == 0 else STREAMS)

    def start(k, stage):
        if not COMM:
            return
        for stream in streams_of(stage):
            exchange(k, stage, stream)[0].start()

    def finish(k, stage):
        if not COMM:
            return
        last = stage == plan.stages
        for stream in streams_of(stage):
            copy, kept, came = exchange(k, stage, stream)
            copy.wait()
            if stage == 0:
                for s in range(STREAMS):
                    for a in range(2):
                        index = (k, s, a) + kept[3:]
                        total = term[index].astype(F32) + stage_in[0][k, s, a].astype(F32)
                        term[index] = total.astype(BF16)
            else:
                total = (term[kept].astype(F32) + came[...].astype(F32)).astype(BF16)
                if last:
                    final[k, :, :, pl.ds(stream * plan.lanes, plan.lanes)] = total
                else:
                    term[kept] = total
            if not last and stage > 0:
                exchange(k, stage + 1, stream)[0].start()
        if stage == 0:
            start(k, 1)
        if last:
            for offset in range(1, plan.space):
                gather(k, offset).start()
            own(k).start()

    def tick(i, static):
        for stage in reversed(range(plan.stages + 1)):
            k = i - 1 - stage
            if static:
                if 0 <= k < K:
                    finish(k, stage)
            else:
                pl.when(k >= 0)(functools.partial(finish, k, stage))

    def late_chunk(k, carry):
        weight_load(k, 0).wait()
        weight_load(k, 1).wait()

        wi = w_in[:, k].reshape(F, width)
        wo = w_out[:, k].reshape(F, width)

        def tile(t, c):
            first = pl.multiple_of(t * pad, pad)
            v = dot(wi, mixed[t], NT)
            h = dot(wo, cot[t], NT)
            act, grad = gelu_slope_parts(v)
            act_t[t] = act.astype(BF16)
            pg_t[t] = (h * grad).astype(BF16)
            return c

        for t in range(rows):
            tile(t, 0)
        tick(k, False)

        def put(a, value):
            value = (value * inv_batch).astype(BF16)
            for s in range(STREAMS):
                part = value[:, s * plan.lanes : (s + 1) * plan.lanes]
                term[k, s, a] = part.reshape(term.shape[3:])

        def against(lhs, rhs):
            total = dot(lhs[0], rhs[0], NN)
            for t in range(1, rows):
                total = total + dot(lhs[t], rhs[t], NN)
            return total

        put(0, against(act_t, cot))
        put(1, against(pg_t, mixed))
        start(k, 0)
        for t in range(rows):
            mix_acc[t] += dot(pg_t[t], wi, TN)
        return carry

    lax.fori_loop(0, K, late_chunk, 0)
    late_loads[1].start()

    def halo_copy(rows_ref, halo, side, which):
        src = rows_ref.at[0 if side == 0 else rows - 1]
        return pltpu.make_async_remote_copy(
            src_ref=src,
            dst_ref=halo.at[1 - side],
            send_sem=hsend_sem.at[which, side],
            recv_sem=hrecv_sem.at[which, 1 - side],
            device_id={"space": spi - 1 if side == 0 else spi + 1},
            device_id_type=MESH,
        )

    def halo_do(rows_ref, halo, which, act):
        if not COMM:
            return
        pl.when(spi > 0)(lambda: act(halo_copy(rows_ref, halo, 0, which), 0))
        pl.when(spi < plan.space - 1)(lambda: act(halo_copy(rows_ref, halo, 1, which), 1))

    def halo_start(rows_ref, halo, which):
        halo_do(rows_ref, halo, which, lambda copy, side: copy.start())

    def halo_wait(rows_ref, halo, which):
        def wait(copy, side):
            copy.wait_send()
            pltpu.make_async_remote_copy(
                src_ref=rows_ref.at[0],
                dst_ref=halo.at[side],
                send_sem=hsend_sem.at[which, side],
                recv_sem=hrecv_sem.at[which, side],
                device_id={"space": spi - 1 if side == 0 else spi + 1},
                device_id_type=MESH,
            ).wait_recv()

        halo_do(rows_ref, halo, which, wait)

    for r in range(rows):
        mix_row[r] = mix_acc[r].astype(BF16)
    halo_start(mix_row, halo_late, 0)
    tick(K, True)
    ticks = iter(range(K + 1, K + plan.stages + 1))

    def next_tick():
        i = next(ticks, None)
        if i is not None:
            tick(i, True)

    def conv(wanted, halo, rows_ref, kernel_ref, base, store, with_taps):
        def block(c, carry):
            lanes = pl.ds(pl.multiple_of(c * LANES, LANES), LANES)
            weights = kernel_ref[:, lanes].astype(F32)
            windows = {}
            sums = [None] * 9
            for i in wanted:
                total = base(i, lanes).astype(F32)
                held = raw_input[i, :, lanes].astype(F32) if with_taps else None
                for lat in range(3):
                    p = i + 2 - lat
                    if p not in windows:
                        if p == 0:
                            row = halo[0, pl.ds(0, cols), lanes]
                        elif p == rows + 1:
                            row = halo[1, pl.ds(0, cols), lanes]
                        else:
                            row = rows_ref[p - 1, pl.ds(0, cols), lanes]
                        windows[p] = [rolled(row.astype(F32), b - 1) for b in range(3)]
                    for lon in range(3):
                        tap = 3 * lat + lon
                        total = total + weights[tap : tap + 1] * windows[p][lon]
                        if with_taps:
                            part = jnp.sum(held * windows[p][lon], axis=0, keepdims=True)
                            sums[tap] = part if sums[tap] is None else sums[tap] + part
                store(i, lanes, total.astype(BF16))
            if with_taps:
                for tap in range(9):
                    taps[tap : tap + 1, lanes] += sums[tap]
            return carry

        lax.fori_loop(0, width // LANES, block, 0)

    loads[2].wait()
    for r in range(rows):
        early[place[r], pl.ds(0, cols)] = raw_one[r]
    late_loads[0].wait()
    hidden = w_late.shape[0]
    E = slope.shape[2]
    steps = hidden // E

    def early_slope(n, carry):
        w = w_late[pl.ds(pl.multiple_of(n * E, E), E)]
        for r in range(rows):
            v = dot(early[r], w, NT)
            slope[n, pl.ds(r * pad, pad)] = gelu_slope_parts(v)[1].astype(BF16)
        return carry

    lax.fori_loop(0, steps // 2, early_slope, 0)
    next_tick()
    lax.fori_loop(steps // 2, steps, early_slope, 0)
    next_tick()
    loads[3].wait()
    taps[...] = jnp.zeros_like(taps)

    def late_base(i, lanes):
        return raw_cot[i, :, lanes]

    def late_store(i, lanes, value):
        grad_two[place[i], pl.ds(0, cols), lanes] = value

    conv(range(1, rows - 1), halo_late, mix_row, kernel_two, late_base, late_store, True)
    halo_wait(mix_row, halo_late, 0)
    conv([0, rows - 1], halo_late, mix_row, kernel_two, late_base, late_store, True)
    taps[...] = taps[...] * inv_batch

    moves = [("dp", b) for b in range(plan.db)] + [("space", b) for b in range(plan.sb)]

    def taps_copy(n):
        axis, bit = moves[n]
        return pltpu.make_async_remote_copy(
            src_ref=taps,
            dst_ref=taps_in.at[n],
            send_sem=tsend_sem.at[n],
            recv_sem=trecv_sem.at[n],
            device_id={axis: flip(where[axis], bit)},
            device_id_type=MESH,
        )

    def taps_step(n):
        if not COMM:
            return
        if 0 < n <= len(moves):
            taps_copy(n - 1).wait()
            taps[...] += taps_in[n - 1]
        if n < len(moves):
            taps_copy(n).start()

    taps_step(0)
    steps_taps = iter(range(1, len(moves) + 1))

    def next_taps():
        n = next(steps_taps, None)
        if n is not None:
            taps_step(n)

    late_loads[1].wait()
    w_out_flat = w_out.reshape(hidden, width)

    def early_group(first, count):
        span = count * pad
        lo = first * pad

        def chunk(n, carry):
            w_o = w_out_flat[pl.ds(pl.multiple_of(n * E, E), E)]
            w_i = w_late[pl.ds(pl.multiple_of(n * E, E), E)]
            h = dot(grad_two[pl.ds(first, count)].reshape(span, width), w_o, NT)
            s = slope[n, pl.ds(lo, span)].astype(F32)
            g = (h * s).astype(BF16)
            back = dot(g, w_i, NN)
            for r in range(count):
                mix_acc[first + r] += back[r * pad : (r + 1) * pad]
            return carry

        for r in range(count):
            mix_acc[first + r] = jnp.zeros(mix_acc.shape[1:], F32)
        lax.fori_loop(0, steps // 2, chunk, 0)
        next_tick()
        next_taps()
        lax.fori_loop(steps // 2, steps, chunk, 0)
        for r in range(count):
            mix_row[order[first + r]] = mix_acc[first + r].astype(BF16)

    early_group(0, 2)
    halo_start(mix_row, halo_early, 1)
    next_tick()
    next_taps()
    early_group(2, rows - 2)
    next_tick()
    next_taps()

    def early_base(i, lanes):
        return grad_two[place[i], pl.ds(0, cols), lanes]

    def early_store(i, lanes, value):
        raw_mixed[i, :, lanes] = value

    def out_copy(i):
        return pltpu.make_async_copy(raw_mixed.at[i], out_ref.at[0, i], out_sem.at[i])

    conv(range(1, rows - 1), halo_early, mix_row, kernel_one, early_base, early_store, False)
    for i in range(1, rows - 1):
        out_copy(i).start()
    for _ in range(plan.stages):
        next_tick()
    halo_wait(mix_row, halo_early, 1)
    conv([0, rows - 1], halo_early, mix_row, kernel_one, early_base, early_store, False)
    out_copy(0).start()
    out_copy(rows - 1).start()
    for _ in moves:
        next_taps()
    taps_out[...] = taps[...]
    if COMM:
        for k in range(K):
            for offset in range(1, plan.space):
                gather(k, offset).wait()
            own(k).wait()
    for i in range(rows):
        out_copy(i).wait()


def whole_call(plan, inv_batch, args):
    mixed_two, input_two, cotangent, w_in_two, w_out_two, kernel_two, mixed_one, w_in_one, w_out_one, kernel_one = args
    _, rows, cols, width = mixed_two.shape
    hidden = w_in_two.shape[0]
    pad = -(-cols // 16) * 16
    K, dp, space, Q = plan.chunks, plan.dp, plan.space, plan.piece
    R = space * Q
    F = dp * R
    E = 512
    w_in_two = w_in_two.reshape(dp, K, R, width)
    w_out_two = w_out_two.reshape(dp, K, R, width)
    w_out_one = w_out_one.reshape(dp, K, R, width)
    anywhere = pl.BlockSpec(memory_space=pl.ANY)
    vmem = pl.BlockSpec(memory_space=pltpu.VMEM)
    stage_shapes = [
        pltpu.VMEM((K, STREAMS, 2) + (2,) * (plan.db + plan.sb - 1 - stage) + (Q, plan.lanes), BF16)
        for stage in range(plan.stages + 1)
    ]
    token = pltpu.VMEM((rows, pad, width), BF16)
    raw = pltpu.VMEM((rows, cols, width), BF16)
    taps = kernel_two.shape[0]
    moves = plan.db + plan.sb
    dma = pltpu.SemaphoreType.DMA
    scratch = [
        raw, raw, raw, raw,
        token, token, token,
        pltpu.VMEM((dp, K, R, width), BF16),
        pltpu.VMEM((dp, K, R, width), BF16),
        pltpu.VMEM((hidden, width), BF16),
        pltpu.VMEM((rows, F, pad), BF16),
        pltpu.VMEM((rows, F, pad), BF16),
        pltpu.VMEM((rows, pad, width), F32),
        token,
        token,
        pltpu.VMEM((hidden // E, rows * pad, E), BF16),
        pltpu.VMEM((2, pad, width), BF16),
        pltpu.VMEM((2, pad, width), BF16),
        pltpu.VMEM((taps, width), F32),
        pltpu.VMEM((moves, taps, width), F32),
        pltpu.VMEM((K, STREAMS, 2) + (2,) * moves + (Q, plan.lanes), BF16),
        pltpu.VMEM((K, 2, Q, width), BF16),
        *stage_shapes,
        dma((4,)), dma((2, K)), dma((2,)), dma((rows,)), dma((K,)),
        dma((K, plan.stages + 1, STREAMS)), dma((K, plan.stages + 1, STREAMS)),
        dma((K, space - 1)), dma((K, space - 1)),
        dma((2, 2)), dma((2, 2)), dma((moves,)), dma((moves,)),
    ]
    return pl.pallas_call(
        functools.partial(kernel, plan, (rows, cols, width), inv_batch),
        in_specs=[anywhere] * 5 + [vmem] + [anywhere] * 3 + [vmem],
        out_specs=[anywhere, anywhere, vmem],
        out_shape=[
            jax.ShapeDtypeStruct(mixed_two.shape, BF16),
            jax.ShapeDtypeStruct((K, space, 2, Q, width), BF16),
            jax.ShapeDtypeStruct((taps, width), F32),
        ],
        scratch_shapes=scratch,
        compiler_params=pltpu.CompilerParams(
            collective_id=0 if COMM else None, has_side_effects=True, vmem_limit_bytes=67_043_328
        ),
    )(mixed_two, input_two, cotangent, w_in_two, w_out_two, kernel_two, mixed_one, w_in_one, w_out_one, kernel_one)


def shards(*args):
    dp, space = lax.axis_size("dp"), lax.axis_size("space")
    samples, width, hidden = args[0].shape[0], args[0].shape[3], args[3].shape[0]
    plan = Plan(dp, space, hidden, width)
    grad_one, grads, taps = whole_call(plan, 1.0 / (samples * dp), args)
    out = grads[:, :, 0].reshape(-1, width).astype(F32)
    inn = grads[:, :, 1].reshape(-1, width).astype(F32)
    return grad_one, inn, out, taps


def solution(mesh):
    tokens = P("dp", "space", None, None)
    return jax.shard_map(
        shards,
        mesh=mesh,
        in_specs=(tokens, tokens, tokens, P(), P(), P(), tokens, P(), P(), P()),
        out_specs=(tokens, P("dp", None), P("dp", None), P()),
        check_vma=False,
    )
```

profile of v0, /device:TPU:0, one launch (start us, length us, event | category | flops | bytes accessed | tf_op | source)
XLA Modules:
  0.0 120.3 jit_solution(14999502487996846343)
XLA Ops:
  0.6 0.0 copy-start.1
  0.6 2.4 %copy.14.mixed_two = bf16[1,4,180,768]{3,2,1,0:T(8,128)(2,1)} copy(bf16[1,4,180,768]{3,1,2,0:T(4,128)(2,1)} %param.10) | data formatting | bytes 2211840 | tf_op args[0]
  3.1 0.0 copy-done.1
  3.1 0.0 copy-start.2
  3.1 1.1 copy.15.input_two
  4.2 0.5 copy-done.2
  4.7 0.0 copy-start.3
  4.7 1.1 copy.16.cotangent
  5.9 0.5 copy-done.3
  6.4 1.1 copy.17.mixed_one
  7.5 107.6 %shard_map.129 = (bf16[1,4,180,768]{3,2,1,0:T(8,128)(2,1)}, bf16[6,4,2,16,768]{4,3,2,1,0:T(8,128)(2,1)}, f32[9,768]{1,0:T(8,128)}) custom-call(bf16[1,4,180,768]{3,2,1,0:T(8,128)(2,1)} %copy.14.mixed_two, bf16[1,4,180,768]{3,2,1,0:T(8,128)(2,1)} %copy.15.input_two, bf16[1,4,180,768]{3,2,1,0:T(8,128)(2,1)} %copy.16.cotangent, ...), custom_call_target="tpu_custom_call" | custom-call | tf_op jit(solution)/shard_map/pallas_call | solution.py:549
  115.1 0.0 copy-start
  115.1 2.8 %copy.18 = bf16[1,4,180,768]{3,1,2,0:T(4,128)(2,1)} copy(bf16[1,4,180,768]{3,2,1,0:T(8,128)(2,1)} %get-tuple-element.10) | data formatting | bytes 2211840
  117.9 0.0 copy-done
  117.9 0.1 fusion
  118.0 0.0 copy-start.4
  118.0 1.7 %bitcast_convert_fusion = (f32[384,768]{1,0:T(8,128)}, f32[384,768]{1,0:T(8,128)}) fusion(bf16[6,4,1,16,768]{4,3,2,1,0:T(8,128)(2,1)S(1)} %get-tuple-element.14, bf16[6,4,1,16,768]{4,3,2,1,0:T(8,128)(2,1)S(1)} %get-tuple-element.15), kind=kLoop, calls=%fused_computation | loop fusion | flops 589824 | bytes 3538944 | tf_op jit(solution)/shard_map/convert_element_type | solution.py:570
  119.7 0.0 copy-done.4
  119.7 0.6 copy.20
Async XLA Ops:
  0.6 2.5 %copy-start.1 = (bf16[1,4,180,768]{3,1,2,0:T(4,128)(2,1)S(1)}, bf16[1,4,180,768]{3,1,2,0:T(4,128)(2,1)}, u32[]{:S(2)}) copy-start(bf16[1,4,180,768]{3,1,2,0:T(4,128)(2,1)} %param.11) | copy-start | bytes 3317764
  3.1 1.7 %copy-start.2 = (bf16[1,4,180,768]{3,1,2,0:T(4,128)(2,1)S(1)}, bf16[1,4,180,768]{3,1,2,0:T(4,128)(2,1)}, u32[]{:S(2)}) copy-start(bf16[1,4,180,768]{3,1,2,0:T(4,128)(2,1)} %param.12) | copy-start | bytes 3317764
  4.7 1.7 %copy-start.3 = (bf16[1,4,180,768]{3,1,2,0:T(4,128)(2,1)S(1)}, bf16[1,4,180,768]{3,1,2,0:T(4,128)(2,1)}, u32[]{:S(2)}) copy-start(bf16[1,4,180,768]{3,1,2,0:T(4,128)(2,1)} %param.16) | copy-start | bytes 3317764
  115.1 2.8 %copy-start = (bf16[6,4,2,16,768]{4,3,2,1,0:T(8,128)(2,1)S(1)}, bf16[6,4,2,16,768]{4,3,2,1,0:T(8,128)(2,1)}, u32[]{:S(2)}) copy-start(bf16[6,4,2,16,768]{4,3,2,1,0:T(8,128)(2,1)} %get-tuple-element.8) | copy-start | bytes 3538948
  118.0 1.7 %copy-start.4 = (f32[9,768]{1,0:T(8,128)S(1)}, f32[9,768]{1,0:T(8,128)}, u32[]{:S(2)}) copy-start(f32[9,768]{1,0:T(8,128)} %get-tuple-element.25) | copy-start | bytes 82948
where the time goes:
time: 121 us; the launch traced here: 120 us
  Pallas kernels  108 us (89%)
  local copies, waits for them, and re-layouts  10.4 us (9%)
  other arithmetic  1.65 us (1%)
    pallas_call x1, Pallas kernels, whole_call(): pl.pallas_call(functools.partial(kernel, plan, (rows, cols, width), inv_b...  108 us
    unnamed x16, local copies, waits for them, and re-layouts  10.3 us

commit v1 on v0

--- a/solution.py
+++ b/solution.py
@@ -17,8 +17,13 @@
 NN = (((1,), (0,)), ((), ()))
 TN = (((0,), (0,)), ((), ()))
 LANES = 128
-STREAMS = 3
+SHARES = (1, 1, 1)
+STREAMS = len(SHARES)
+LAGS = (0, 0, 1)
+FREE, HELD, OPEN = 3, 5, 9
 COMM = True
+WEIGHTS = True
+HALO = True
 
 
 def dot(a, b, dims):
@@ -62,10 +67,12 @@
         rows = hidden // (dp * space)
         self.piece = next(q for q in (16, 8, rows) if rows % q == 0)
         self.chunks = rows // self.piece
-        self.lanes = width // STREAMS
+        unit = width // sum(SHARES)
+        self.lanes = [unit * share for share in SHARES]
+        self.first = [unit * sum(SHARES[:n]) for n in range(STREAMS)]
         spaces = [("space", b) for b in range(self.sb)]
         rest = [("dp", b) for b in range(1, self.db)]
-        self.orders = [spaces + rest, spaces[::-1] + rest, rest + spaces]
+        self.orders = [spaces + rest, spaces[::-1] + rest, rest + spaces[::-1]]
         self.stages = self.sb + self.db - 1
 
     def labels(self):
@@ -78,18 +85,22 @@
     plan, shape, inv_batch,
     mixed_two, input_two, cotangent, w_in_two, w_out_two, kernel_two, mixed_one, w_in_one, w_out_one, kernel_one,
     out_ref, grads_ref, taps_out,
-    raw_mixed, raw_input, raw_cot, raw_one,
+    raw_mixed, raw_input, raw_cot, raw_one, input_row,
     mixed, cot, early, w_in, w_out, w_late, act_t, pg_t, mix_acc, mix_row, grad_two, slope,
-    halo_late, halo_early, taps, taps_in, term, final, *rest,
+    halo_late, halo_early, taps, taps_in, gathered, *rest,
 ):
-    stage_in = rest[: plan.stages + 1]
+    count = (plan.stages + 1) * STREAMS
+    term = rest[:STREAMS]
+    stage_in = [rest[STREAMS + n : STREAMS + count : STREAMS] for n in range(STREAMS)]
+    rest = rest[STREAMS + count :]
     (
         load_sem, weight_sem, late_sem, out_sem, own_sem,
         send_sem, recv_sem, gsend_sem, grecv_sem, hsend_sem, hrecv_sem, tsend_sem, trecv_sem,
-    ) = rest[plan.stages + 1 :]
+    ) = rest
     rows, cols, width = shape
-    pad = mixed.shape[1]
-    tokens = rows * pad
+    tokens = mixed.shape[0]
+    pad = tokens // rows
+    T = act_t.shape[2]
     K = plan.chunks
     F = w_in.shape[0] * w_in.shape[2]
     dpi, spi = lax.axis_index("dp"), lax.axis_index("space")
@@ -141,8 +152,8 @@
 
     zeros = jnp.zeros((16, width), BF16)
     for r in range(rows):
-        mixed[r, pl.ds(pad - 16, 16)] = zeros
-        cot[r, pl.ds(pad - 16, 16)] = zeros
+        mixed[pl.ds((r + 1) * pad - 16, 16)] = zeros
+        cot[pl.ds((r + 1) * pad - 16, 16)] = zeros
         early[r, pl.ds(pad - 16, 16)] = zeros
         grad_two[r, pl.ds(pad - 16, 16)] = zeros
     mix_acc[...] = jnp.zeros_like(mix_acc)
@@ -150,15 +161,12 @@
         pl.when(spi == 0)(lambda halo=halo: halo.__setitem__(0, jnp.zeros(halo.shape[1:], BF16)))
         pl.when(spi == plan.space - 1)(lambda halo=halo: halo.__setitem__(1, jnp.zeros(halo.shape[1:], BF16)))
 
-    if COMM:
-        pl.semaphore_wait(barrier, len(peers))
-
     loads[0].wait()
     for r in range(rows):
-        mixed[r, pl.ds(0, cols)] = raw_mixed[r]
+        mixed[pl.ds(r * pad, cols)] = raw_mixed[:, r, :]
     loads[1].wait()
     for r in range(rows):
-        cot[r, pl.ds(0, cols)] = raw_cot[r]
+        cot[pl.ds(r * pad, cols)] = raw_cot[:, r, :]
 
     def half(done, now, value):
         index = []
@@ -172,84 +180,115 @@
         return tuple(index)
 
     def exchange(k, stage, stream):
-        if stage == 0:
-            now, done, streams = ("dp", 0), [], slice(None)
-            dst = stage_in[0].at[k]
-        else:
-            now = plan.orders[stream][stage - 1]
-            done, streams = [("dp", 0)] + plan.orders[stream][: stage - 1], stream
-            dst = stage_in[stage].at[k, stream]
+        now = ("dp", 0) if stage == 0 else plan.orders[stream][stage - 1]
+        done = ([("dp", 0)] + plan.orders[stream])[:stage]
         mine = my_bit(where[now[0]], now[1])
-        src = term.at[(k, streams, slice(None)) + half(done, now, 1 - mine)]
-        kept = (k, streams, slice(None)) + half(done, now, mine)
+        kept = (k, slice(None)) + half(done, now, mine)
+        came = stage_in[stream][stage].at[k]
         copy = pltpu.make_async_remote_copy(
-            src_ref=src,
-            dst_ref=dst,
+            src_ref=term[stream].at[(k, slice(None)) + half(done, now, 1 - mine)],
+            dst_ref=came,
             send_sem=send_sem.at[k, stage, stream],
             recv_sem=recv_sem.at[k, stage, stream],
             device_id={now[0]: flip(where[now[0]], now[1])},
             device_id_type=MESH,
         )
-        return copy, kept, dst
-
-    def gather(k, offset):
+        return copy, kept, came
+
+    def gather(k, bit):
+        pieces = gathered.at[k, pl.ds(spi // (1 << bit) * (1 << bit), 1 << bit)]
         return pltpu.make_async_remote_copy(
-            src_ref=final.at[k],
-            dst_ref=grads_ref.at[k, spi],
-            send_sem=gsend_sem.at[k, offset - 1],
-            recv_sem=grecv_sem.at[k, offset - 1],
-            device_id={"space": across(offset)},
+            src_ref=pieces,
+            dst_ref=pieces,
+            send_sem=gsend_sem.at[k, bit],
+            recv_sem=grecv_sem.at[k, bit],
+            device_id={"space": flip(spi, bit)},
             device_id_type=MESH,
         )
 
     def own(k):
-        return pltpu.make_async_copy(final.at[k], grads_ref.at[k, spi], own_sem.at[k])
-
-    def streams_of(stage):
-        return range(1 if stage == 0 else STREAMS)
+        return pltpu.make_async_copy(gathered.at[k], grads_ref.at[k], own_sem.at[k])
 
     def start(k, stage):
-        if not COMM:
+        if not (COMM and WEIGHTS):
             return
-        for stream in streams_of(stage):
+        for stream in range(STREAMS):
             exchange(k, stage, stream)[0].start()
 
-    def finish(k, stage):
-        if not COMM:
+    def finish(k, stage, stream):
+        if not (COMM and WEIGHTS):
             return
-        last = stage == plan.stages
-        for stream in streams_of(stage):
-            copy, kept, came = exchange(k, stage, stream)
-            copy.wait()
-            if stage == 0:
-                for s in range(STREAMS):
-                    for a in range(2):
-                        index = (k, s, a) + kept[3:]
-                        total = term[index].astype(F32) + stage_in[0][k, s, a].astype(F32)
-                        term[index] = total.astype(BF16)
+        copy, kept, came = exchange(k, stage, stream)
+        copy.wait()
+        if stage == 0:
+            for a in range(2):
+                index = (k, a) + kept[2:]
+                total = term[stream][index].astype(F32) + came[a].astype(F32)
+                term[stream][index] = total.astype(BF16)
+        else:
+            total = (term[stream][kept].astype(F32) + came[...].astype(F32)).astype(BF16)
+            if stage == plan.stages:
+                gathered[k, spi, :, :, pl.ds(plan.first[stream], plan.lanes[stream])] = total
             else:
-                total = (term[kept].astype(F32) + came[...].astype(F32)).astype(BF16)
-                if last:
-                    final[k, :, :, pl.ds(stream * plan.lanes, plan.lanes)] = total
+                term[stream][kept] = total
+        if stage < plan.stages:
+            exchange(k, stage + 1, stream)[0].start()
+
+    def spread_out(k, bit):
+        if not (COMM and WEIGHTS):
+            return
+        if bit >= 0:
+            gather(k, bit).wait()
+        if bit + 1 < plan.sb:
+            gather(k, bit + 1).start()
+        else:
+            own(k).start()
+
+    def tick(i):
+        for stage in reversed(range(plan.stages + 1)):
+            for stream in range(STREAMS):
+                back = i - 1 - stage - (LAGS[stream] if stage > 0 else 0)
+                if stage + 1 + (LAGS[stream] if stage > 0 else 0) < K:
+                    pl.when(back >= 0)(functools.partial(finish, back, stage, stream))
+
+    left = {}
+    for k in range(K):
+        for stream in range(STREAMS):
+            done = K - 1 - k
+            later = max(0, min(plan.stages, done - 1 - LAGS[stream]))
+            left[k, stream] = [min(done, 1) + later, -1]
+        left[k, STREAMS] = [plan.stages + 1, None]
+
+    def axis_of(stage, stream):
+        if stream == STREAMS:
+            return ("space", stage - plan.stages - 1)
+        return ("dp", 0) if stage == 0 else plan.orders[stream][stage - 1]
+
+    def slot(j):
+        for k in range(K):
+            for stream in range(STREAMS + 1):
+                stage, began = left[k, stream]
+                if stream == STREAMS:
+                    if began is None and all(left[k, n][0] > plan.stages for n in range(STREAMS)):
+                        spread_out(k, -1)
+                        left[k, stream][1] = j
+                        continue
+                    if began is None or stage > plan.stages + plan.sb:
+                        continue
+                elif stage > plan.stages:
+                    continue
+                if began >= j:
+                    continue
+                axis, bit = axis_of(stage, stream)
+                if axis == "space" and j < (FREE if began < HELD else OPEN):
+                    continue
+                if stream == STREAMS and j < (OPEN if bit > 0 or began >= HELD else HELD):
+                    continue
+                if stream == STREAMS:
+                    spread_out(k, stage - plan.stages - 1)
                 else:
-                    term[kept] = total
-            if not last and stage > 0:
-                exchange(k, stage + 1, stream)[0].start()
-        if stage == 0:
-            start(k, 1)
-        if last:
-            for offset in range(1, plan.space):
-                gather(k, offset).start()
-            own(k).start()
-
-    def tick(i, static):
-        for stage in reversed(range(plan.stages + 1)):
-            k = i - 1 - stage
-            if static:
-                if 0 <= k < K:
-                    finish(k, stage)
-            else:
-                pl.when(k >= 0)(functools.partial(finish, k, stage))
+                    finish(k, stage, stream)
+                left[k, stream] = [stage + 1, j]
 
     def late_chunk(k, carry):
         weight_load(k, 0).wait()
@@ -259,39 +298,44 @@
         wo = w_out[:, k].reshape(F, width)
 
         def tile(t, c):
-            first = pl.multiple_of(t * pad, pad)
-            v = dot(wi, mixed[t], NT)
-            h = dot(wo, cot[t], NT)
+            v = dot(wi, mixed[pl.ds(t * T, T)], NT)
+            h = dot(wo, cot[pl.ds(t * T, T)], NT)
             act, grad = gelu_slope_parts(v)
             act_t[t] = act.astype(BF16)
             pg_t[t] = (h * grad).astype(BF16)
             return c
 
-        for t in range(rows):
+        for t in range(tokens // T):
             tile(t, 0)
-        tick(k, False)
+        if COMM:
+            pl.when(k == 0)(lambda: pl.semaphore_wait(barrier, len(peers)))
+        for t in range(tokens // T):
+            mix_acc[pl.ds(t * T, T)] += dot(pg_t[t], wi, TN)
+
+        @pl.when(k == K - 1)
+        def _():
+            for r in range(rows):
+                mix_row[r] = mix_acc[pl.ds(r * pad, cols)].astype(BF16)
+            halo_start(mix_row, halo_late, 0)
+
+        tick(k)
 
         def put(a, value):
             value = (value * inv_batch).astype(BF16)
             for s in range(STREAMS):
-                part = value[:, s * plan.lanes : (s + 1) * plan.lanes]
-                term[k, s, a] = part.reshape(term.shape[3:])
+                part = value[:, plan.first[s] : plan.first[s] + plan.lanes[s]]
+                term[s][k, a] = part.reshape(term[s].shape[2:])
 
         def against(lhs, rhs):
-            total = dot(lhs[0], rhs[0], NN)
-            for t in range(1, rows):
-                total = total + dot(lhs[t], rhs[t], NN)
+            total = dot(lhs[0], rhs[pl.ds(0, T)], NN)
+            for t in range(1, tokens // T):
+                total = total + dot(lhs[t], rhs[pl.ds(t * T, T)], NN)
             return total
 
         put(0, against(act_t, cot))
         put(1, against(pg_t, mixed))
         start(k, 0)
-        for t in range(rows):
-            mix_acc[t] += dot(pg_t[t], wi, TN)
         return carry
-
-    lax.fori_loop(0, K, late_chunk, 0)
-    late_loads[1].start()
 
     def halo_copy(rows_ref, halo, side, which):
         src = rows_ref.at[0 if side == 0 else rows - 1]
@@ -305,7 +349,7 @@
         )
 
     def halo_do(rows_ref, halo, which, act):
-        if not COMM:
+        if not (COMM and HALO):
             return
         pl.when(spi > 0)(lambda: act(halo_copy(rows_ref, halo, 0, which), 0))
         pl.when(spi < plan.space - 1)(lambda: act(halo_copy(rows_ref, halo, 1, which), 1))
@@ -327,16 +371,12 @@
 
         halo_do(rows_ref, halo, which, wait)
 
-    for r in range(rows):
-        mix_row[r] = mix_acc[r].astype(BF16)
-    halo_start(mix_row, halo_late, 0)
-    tick(K, True)
-    ticks = iter(range(K + 1, K + plan.stages + 1))
+    lax.fori_loop(0, K, late_chunk, 0)
+    late_loads[1].start()
+    slots = iter(range(64))
 
     def next_tick():
-        i = next(ticks, None)
-        if i is not None:
-            tick(i, True)
+        slot(next(slots))
 
     def conv(wanted, halo, rows_ref, kernel_ref, base, store, with_taps):
         def block(c, carry):
@@ -346,16 +386,16 @@
             sums = [None] * 9
             for i in wanted:
                 total = base(i, lanes).astype(F32)
-                held = raw_input[i, :, lanes].astype(F32) if with_taps else None
+                held = input_row[i, :, lanes].astype(F32) if with_taps else None
                 for lat in range(3):
                     p = i + 2 - lat
                     if p not in windows:
                         if p == 0:
-                            row = halo[0, pl.ds(0, cols), lanes]
+                            row = halo[0, :, lanes]
                         elif p == rows + 1:
-                            row = halo[1, pl.ds(0, cols), lanes]
+                            row = halo[1, :, lanes]
                         else:
-                            row = rows_ref[p - 1, pl.ds(0, cols), lanes]
+                            row = rows_ref[p - 1, :, lanes]
                         windows[p] = [rolled(row.astype(F32), b - 1) for b in range(3)]
                     for lon in range(3):
                         tap = 3 * lat + lon
@@ -373,7 +413,7 @@
 
     loads[2].wait()
     for r in range(rows):
-        early[place[r], pl.ds(0, cols)] = raw_one[r]
+        early[place[r], pl.ds(0, cols)] = raw_one[:, r, :]
     late_loads[0].wait()
     hidden = w_late.shape[0]
     E = slope.shape[2]
@@ -381,9 +421,9 @@
 
     def early_slope(n, carry):
         w = w_late[pl.ds(pl.multiple_of(n * E, E), E)]
-        for r in range(rows):
-            v = dot(early[r], w, NT)
-            slope[n, pl.ds(r * pad, pad)] = gelu_slope_parts(v)[1].astype(BF16)
+        for r in range(0, rows, 2):
+            v = dot(early[pl.ds(r, 2)].reshape(2 * pad, width), w, NT)
+            slope[n, pl.ds(r * pad, 2 * pad)] = gelu_slope_parts(v)[1].astype(BF16)
         return carry
 
     lax.fori_loop(0, steps // 2, early_slope, 0)
@@ -391,20 +431,23 @@
     lax.fori_loop(steps // 2, steps, early_slope, 0)
     next_tick()
     loads[3].wait()
+    for r in range(rows):
+        input_row[r] = raw_input[:, r, :]
     taps[...] = jnp.zeros_like(taps)
 
     def late_base(i, lanes):
-        return raw_cot[i, :, lanes]
+        return cot[pl.ds(i * pad, cols), lanes]
 
     def late_store(i, lanes, value):
         grad_two[place[i], pl.ds(0, cols), lanes] = value
 
     conv(range(1, rows - 1), halo_late, mix_row, kernel_two, late_base, late_store, True)
+    next_tick()
     halo_wait(mix_row, halo_late, 0)
     conv([0, rows - 1], halo_late, mix_row, kernel_two, late_base, late_store, True)
     taps[...] = taps[...] * inv_batch
 
-    moves = [("dp", b) for b in range(plan.db)] + [("space", b) for b in range(plan.sb)]
+    moves = [("space", b) for b in range(plan.sb)] + [("dp", b) for b in range(plan.db)]
 
     def taps_copy(n):
         axis, bit = moves[n]
@@ -418,7 +461,7 @@
         )
 
     def taps_step(n):
-        if not COMM:
+        if not (COMM and HALO):
             return
         if 0 < n <= len(moves):
             taps_copy(n - 1).wait()
@@ -427,6 +470,7 @@
             taps_copy(n).start()
 
     taps_step(0)
+    next_tick()
     steps_taps = iter(range(1, len(moves) + 1))
 
     def next_taps():
@@ -449,51 +493,51 @@
             g = (h * s).astype(BF16)
             back = dot(g, w_i, NN)
             for r in range(count):
-                mix_acc[first + r] += back[r * pad : (r + 1) * pad]
+                mix_acc[pl.ds((first + r) * pad, pad)] += back[r * pad : (r + 1) * pad]
             return carry
 
         for r in range(count):
-            mix_acc[first + r] = jnp.zeros(mix_acc.shape[1:], F32)
+            mix_acc[pl.ds((first + r) * pad, pad)] = jnp.zeros((pad, width), F32)
         lax.fori_loop(0, steps // 2, chunk, 0)
+        next_taps()
         next_tick()
-        next_taps()
         lax.fori_loop(steps // 2, steps, chunk, 0)
         for r in range(count):
-            mix_row[order[first + r]] = mix_acc[first + r].astype(BF16)
+            mix_row[order[first + r]] = mix_acc[pl.ds((first + r) * pad, cols)].astype(BF16)
 
     early_group(0, 2)
     halo_start(mix_row, halo_early, 1)
-    next_tick()
     next_taps()
+    next_tick()
     early_group(2, rows - 2)
-    next_tick()
     next_taps()
+    next_tick()
 
     def early_base(i, lanes):
         return grad_two[place[i], pl.ds(0, cols), lanes]
 
     def early_store(i, lanes, value):
-        raw_mixed[i, :, lanes] = value
+        input_row[i, :, lanes] = value
 
     def out_copy(i):
-        return pltpu.make_async_copy(raw_mixed.at[i], out_ref.at[0, i], out_sem.at[i])
+        return pltpu.make_async_copy(input_row.at[i], out_ref.at[0, i], out_sem.at[i])
 
     conv(range(1, rows - 1), halo_early, mix_row, kernel_one, early_base, early_store, False)
     for i in range(1, rows - 1):
         out_copy(i).start()
-    for _ in range(plan.stages):
-        next_tick()
+    next_tick()
     halo_wait(mix_row, halo_early, 1)
+    next_tick()
     conv([0, rows - 1], halo_early, mix_row, kernel_one, early_base, early_store, False)
     out_copy(0).start()
     out_copy(rows - 1).start()
+    for _ in range(plan.stages + plan.sb + 1):
+        next_tick()
     for _ in moves:
         next_taps()
     taps_out[...] = taps[...]
-    if COMM:
+    if COMM and WEIGHTS:
         for k in range(K):
-            for offset in range(1, plan.space):
-                gather(k, offset).wait()
             own(k).wait()
     for i in range(rows):
         out_copy(i).wait()
@@ -508,42 +552,51 @@
     R = space * Q
     F = dp * R
     E = 512
+    tokens = rows * pad
+    T = next(t for t in (256, pad) if tokens % t == 0)
     w_in_two = w_in_two.reshape(dp, K, R, width)
     w_out_two = w_out_two.reshape(dp, K, R, width)
     w_out_one = w_out_one.reshape(dp, K, R, width)
+
+    def turned(x):
+        return jnp.transpose(x, (0, 2, 1, 3))
+
     anywhere = pl.BlockSpec(memory_space=pl.ANY)
     vmem = pl.BlockSpec(memory_space=pltpu.VMEM)
-    stage_shapes = [
-        pltpu.VMEM((K, STREAMS, 2) + (2,) * (plan.db + plan.sb - 1 - stage) + (Q, plan.lanes), BF16)
-        for stage in range(plan.stages + 1)
+    bits = plan.db + plan.sb
+    piece_shapes = [
+        pltpu.VMEM((K, 2) + (2,) * (bits - step) + (Q, lanes), BF16)
+        for step in range(bits + 1)
+        for lanes in plan.lanes
     ]
     token = pltpu.VMEM((rows, pad, width), BF16)
+    flat = pltpu.VMEM((tokens, width), BF16)
+    lying = pltpu.VMEM((cols, rows, width), BF16)
     raw = pltpu.VMEM((rows, cols, width), BF16)
     taps = kernel_two.shape[0]
     moves = plan.db + plan.sb
     dma = pltpu.SemaphoreType.DMA
     scratch = [
-        raw, raw, raw, raw,
-        token, token, token,
+        lying, lying, lying, lying, raw,
+        flat, flat, token,
         pltpu.VMEM((dp, K, R, width), BF16),
         pltpu.VMEM((dp, K, R, width), BF16),
         pltpu.VMEM((hidden, width), BF16),
-        pltpu.VMEM((rows, F, pad), BF16),
-        pltpu.VMEM((rows, F, pad), BF16),
-        pltpu.VMEM((rows, pad, width), F32),
-        token,
+        pltpu.VMEM((tokens // T, F, T), BF16),
+        pltpu.VMEM((tokens // T, F, T), BF16),
+        pltpu.VMEM((tokens, width), F32),
+        raw,
         token,
         pltpu.VMEM((hidden // E, rows * pad, E), BF16),
-        pltpu.VMEM((2, pad, width), BF16),
-        pltpu.VMEM((2, pad, width), BF16),
+        pltpu.VMEM((2, cols, width), BF16),
+        pltpu.VMEM((2, cols, width), BF16),
         pltpu.VMEM((taps, width), F32),
         pltpu.VMEM((moves, taps, width), F32),
-        pltpu.VMEM((K, STREAMS, 2) + (2,) * moves + (Q, plan.lanes), BF16),
-        pltpu.VMEM((K, 2, Q, width), BF16),
-        *stage_shapes,
+        pltpu.VMEM((K, space, 2, Q, width), BF16),
+        *piece_shapes,
         dma((4,)), dma((2, K)), dma((2,)), dma((rows,)), dma((K,)),
         dma((K, plan.stages + 1, STREAMS)), dma((K, plan.stages + 1, STREAMS)),
-        dma((K, space - 1)), dma((K, space - 1)),
+        dma((K, plan.sb)), dma((K, plan.sb)),
         dma((2, 2)), dma((2, 2)), dma((moves,)), dma((moves,)),
     ]
     return pl.pallas_call(
@@ -559,7 +612,10 @@
         compiler_params=pltpu.CompilerParams(
             collective_id=0 if COMM else None, has_side_effects=True, vmem_limit_bytes=67_043_328
         ),
-    )(mixed_two, input_two, cotangent, w_in_two, w_out_two, kernel_two, mixed_one, w_in_one, w_out_one, kernel_one)
+    )(
+        turned(mixed_two), turned(input_two), turned(cotangent), w_in_two, w_out_two, kernel_two,
+        turned(mixed_one), w_in_one, w_out_one, kernel_one,
+    )
 
 
 def shards(*args):

time: 121 us -> 104 us (0.86)
  Pallas kernels: 108 us -> 98 us
  local copies, waits for them, and re-layouts: 10.4 us -> 3.51 us
    pallas_call x1, Pallas kernels: 108 us -> 98 us  [whole_call(): pl.pallas_call(functools.partial(kernel, plan, (rows, cols, width), inv_b...]
    unnamed x16 -> x6, local copies, waits for them, and re-layouts: 10.3 us -> 3.39 us
where the time goes in v1:
time: 104 us
  Pallas kernels  98 us (94%)
  local copies, waits for them, and re-layouts  3.51 us (3%)
  other arithmetic  1.65 us (2%)
    pallas_call x1, Pallas kernels, whole_call(): pl.pallas_call(functools.partial(kernel, plan, (rows, cols, width), inv_b...  98 us
    unnamed x6, local copies, waits for them, and re-layouts  3.39 us

profile of v1, /device:TPU:0, one launch (start us, length us, event | category | flops | bytes accessed | tf_op | source)
XLA Modules:
  0.0 103.8 jit_solution(12681547033399093367)
XLA Ops:
  0.6 98.0 %shard_map.129 = (bf16[1,4,180,768]{3,2,1,0:T(8,128)(2,1)}, bf16[6,4,2,16,768]{4,3,2,1,0:T(8,128)(2,1)}, f32[9,768]{1,0:T(8,128)}) custom-call(bf16[1,180,4,768]{3,2,1,0:T(4,128)(2,1)} %bitcast.16, bf16[1,180,4,768]{3,2,1,0:T(4,128)(2,1)} %bitcast.17, bf16[1,180,4,768]{3,2,1,0:T(4,128)(2,1)} %bitcast.18, bf16[8,6,64,768]{3,2,1,0:T(8,128)(2,1)} %bitcast.13, ...), custom_call_target="tpu_custom_call" | custom-call | tf_op jit(solution)/shard_map/pallas_call | solution.py:602
  98.6 0.0 copy-start
  98.6 2.8 %copy.14 = bf16[1,4,180,768]{3,1,2,0:T(4,128)(2,1)} copy(bf16[1,4,180,768]{3,2,1,0:T(8,128)(2,1)} %get-tuple-element.10) | data formatting | bytes 2211840
  101.4 0.0 copy-done
  101.4 0.1 fusion
  101.5 0.0 copy-start.1
  101.5 1.7 %bitcast_convert_fusion = (f32[384,768]{1,0:T(8,128)}, f32[384,768]{1,0:T(8,128)}) fusion(bf16[6,4,1,16,768]{4,3,2,1,0:T(8,128)(2,1)S(1)} %get-tuple-element.14, bf16[6,4,1,16,768]{4,3,2,1,0:T(8,128)(2,1)S(1)} %get-tuple-element.15), kind=kLoop, calls=%fused_computation | loop fusion | flops 589824 | bytes 3538944 | tf_op jit(solution)/shard_map/convert_element_type | solution.py:626
  103.2 0.0 copy-done.1
  103.2 0.6 copy.16
Async XLA Ops:
  98.6 2.8 %copy-start = (bf16[6,4,2,16,768]{4,3,2,1,0:T(8,128)(2,1)S(1)}, bf16[6,4,2,16,768]{4,3,2,1,0:T(8,128)(2,1)}, u32[]{:S(2)}) copy-start(bf16[6,4,2,16,768]{4,3,2,1,0:T(8,128)(2,1)} %get-tuple-element.8) | copy-start | bytes 3538948
  101.5 1.7 %copy-start.1 = (f32[9,768]{1,0:T(8,128)S(1)}, f32[9,768]{1,0:T(8,128)}, u32[]{:S(2)}) copy-start(f32[9,768]{1,0:T(8,128)} %get-tuple-element.25) | copy-start | bytes 82948

commit v2 on v1

--- a/solution.py
+++ b/solution.py
@@ -20,7 +20,7 @@
 SHARES = (1, 1, 1)
 STREAMS = len(SHARES)
 LAGS = (0, 0, 1)
-FREE, HELD, OPEN = 3, 5, 9
+FREE, HELD, OPEN, END = 2, 4, 7, 9
 COMM = True
 WEIGHTS = True
 HALO = True
@@ -279,10 +279,12 @@
                     continue
                 if began >= j:
                     continue
+                if 0 <= began and j - began < (2 if k < K - 1 and j < 3 and stream < STREAMS else 1):
+                    continue
                 axis, bit = axis_of(stage, stream)
                 if axis == "space" and j < (FREE if began < HELD else OPEN):
                     continue
-                if stream == STREAMS and j < (OPEN if bit > 0 or began >= HELD else HELD):
+                if stream == STREAMS and j < (END if bit > 0 else OPEN if began >= HELD else HELD):
                     continue
                 if stream == STREAMS:
                     spread_out(k, stage - plan.stages - 1)
@@ -419,16 +421,16 @@
     E = slope.shape[2]
     steps = hidden // E
 
-    def early_slope(n, carry):
-        w = w_late[pl.ds(pl.multiple_of(n * E, E), E)]
-        for r in range(0, rows, 2):
-            v = dot(early[pl.ds(r, 2)].reshape(2 * pad, width), w, NT)
-            slope[n, pl.ds(r * pad, 2 * pad)] = gelu_slope_parts(v)[1].astype(BF16)
-        return carry
-
-    lax.fori_loop(0, steps // 2, early_slope, 0)
-    next_tick()
-    lax.fori_loop(steps // 2, steps, early_slope, 0)
+    def early_slope(first, count):
+        def step(n, carry):
+            w = w_late[pl.ds(pl.multiple_of(n * E, E), E)]
+            v = dot(early[pl.ds(first, count)].reshape(count * pad, width), w, NT)
+            slope[n, pl.ds(first * pad, count * pad)] = gelu_slope_parts(v)[1].astype(BF16)
+            return carry
+
+        lax.fori_loop(0, steps, step, 0)
+
+    early_slope(0, 2)
     next_tick()
     loads[3].wait()
     for r in range(rows):
@@ -509,8 +511,10 @@
     halo_start(mix_row, halo_early, 1)
     next_taps()
     next_tick()
+    early_slope(2, rows - 2)
+    next_taps()
+    next_tick()
     early_group(2, rows - 2)
-    next_taps()
     next_tick()
 
     def early_base(i, lanes):
@@ -527,12 +531,12 @@
         out_copy(i).start()
     next_tick()
     halo_wait(mix_row, halo_early, 1)
-    next_tick()
     conv([0, rows - 1], halo_early, mix_row, kernel_one, early_base, early_store, False)
     out_copy(0).start()
     out_copy(rows - 1).start()
     for _ in range(plan.stages + plan.sb + 1):
         next_tick()
+    assert all(stage == plan.stages + 1 + (plan.sb if n == STREAMS else 0) for (_, n), (stage, _) in left.items())
     for _ in moves:
         next_taps()
     taps_out[...] = taps[...]

time: 104 us -> 97.1 us (0.934)
  Pallas kernels: 98 us -> 91 us
    pallas_call x1, Pallas kernels: 98 us -> 91 us  [whole_call(): pl.pallas_call(functools.partial(kernel, plan, (rows, cols, width), inv_b...]
where the time goes in v2:
time: 97.1 us; the launch traced here: 96.9 us
  Pallas kernels  91 us (94%)
  local copies, waits for them, and re-layouts  3.51 us (4%)
  other arithmetic  1.65 us (2%)
    pallas_call x1, Pallas kernels, whole_call(): pl.pallas_call(functools.partial(kernel, plan, (rows, cols, width), inv_b...  91 us
    unnamed x6, local copies, waits for them, and re-layouts  3.39 us

profile of v2, /device:TPU:0, one launch (start us, length us, event | category | flops | bytes accessed | tf_op | source)
XLA Modules:
  0.0 96.9 jit_solution(11873531617198078680)
XLA Ops:
  0.6 91.0 %shard_map.129 = (bf16[1,4,180,768]{3,2,1,0:T(8,128)(2,1)}, bf16[6,4,2,16,768]{4,3,2,1,0:T(8,128)(2,1)}, f32[9,768]{1,0:T(8,128)}) custom-call(bf16[1,180,4,768]{3,2,1,0:T(4,128)(2,1)} %bitcast.16, bf16[1,180,4,768]{3,2,1,0:T(4,128)(2,1)} %bitcast.17, bf16[1,180,4,768]{3,2,1,0:T(4,128)(2,1)} %bitcast.18, bf16[8,6,64,768]{3,2,1,0:T(8,128)(2,1)} %bitcast.13, ...), custom_call_target="tpu_custom_call" | custom-call | tf_op jit(solution)/shard_map/pallas_call | solution.py:606
  91.7 0.0 copy-start
  91.7 2.8 %copy.14 = bf16[1,4,180,768]{3,1,2,0:T(4,128)(2,1)} copy(bf16[1,4,180,768]{3,2,1,0:T(8,128)(2,1)} %get-tuple-element.10) | data formatting | bytes 2211840
  94.5 0.0 copy-done
  94.5 0.1 fusion
  94.6 0.0 copy-start.1
  94.6 1.7 %bitcast_convert_fusion = (f32[384,768]{1,0:T(8,128)}, f32[384,768]{1,0:T(8,128)}) fusion(bf16[6,4,1,16,768]{4,3,2,1,0:T(8,128)(2,1)S(1)} %get-tuple-element.14, bf16[6,4,1,16,768]{4,3,2,1,0:T(8,128)(2,1)S(1)} %get-tuple-element.15), kind=kLoop, calls=%fused_computation | loop fusion | flops 589824 | bytes 3538944 | tf_op jit(solution)/shard_map/convert_element_type | solution.py:630
  96.2 0.0 copy-done.1
  96.2 0.6 copy.16
Async XLA Ops:
  91.7 2.8 %copy-start = (bf16[6,4,2,16,768]{4,3,2,1,0:T(8,128)(2,1)S(1)}, bf16[6,4,2,16,768]{4,3,2,1,0:T(8,128)(2,1)}, u32[]{:S(2)}) copy-start(bf16[6,4,2,16,768]{4,3,2,1,0:T(8,128)(2,1)} %get-tuple-element.8) | copy-start | bytes 3538948
  94.6 1.7 %copy-start.1 = (f32[9,768]{1,0:T(8,128)S(1)}, f32[9,768]{1,0:T(8,128)}, u32[]{:S(2)}) copy-start(f32[9,768]{1,0:T(8,128)} %get-tuple-element.25) | copy-start | bytes 82948
